TPU v7x, 32 devices: a whole 2x2x4 slice. The times are simulated.
32 devices in a mesh: clients: 8 (over y, x, core), shard: 4 (over z).
Axes of the slice: x: 2, y: 2, z: 4, core: 2. Of those that a mesh axis runs over, the one named last changes fastest.
Arguments:
- client_deltas: bfloat16 [64, 32, 3584], P(('clients', 'shard')), may hold values from -6 to 6
- variate_deltas: bfloat16 [64, 32, 3584], P(('clients', 'shard')), may hold values from -6 to 6
- params: float32 [32, 3584], P(('clients', 'shard')), may hold values from -1.5 to 1.5
- variate: float32 [32, 3584], P(('clients', 'shard')), may hold values from -1.5 to 1.5
- taking_part: int32 [64], P(('clients', 'shard')), may hold values from 0 to 1, as said below
- counts: int32 [64], P(('clients', 'shard')), may hold values from 32 to 285
Outputs:
- new_params: float32 [32, 3584], P(('clients', 'shard'))
- new_variate: float32 [32, 3584], P(('clients', 'shard'))
- client_params: bfloat16 [32, 3584], replicated
- client_variate: bfloat16 [32, 3584], replicated
Inputs may be any that keep to these rules, and one draw needn't show every extreme that they name: `taking_part`: at least one client takes part.
All inputs are finite; a program needn't handle non-finite values.
Results may differ from a plain program's by a relative error of at most 0.001.
Values may be sent and summed in bfloat16 or wider, within the bound.
A program may use at most 64 MiB of HBM per device.

v0:
```python
import jax
import jax.numpy as jnp
from jax import lax
from jax.sharding import PartitionSpec as P


def weight_rows(taking_part, counts):
    weight = taking_part * counts
    upper_part = weight // 16 * 16
    lower_part = weight - upper_part
    weight_table = jnp.stack([upper_part, lower_part]).astype(jnp.bfloat16)
    chosen = taking_part.astype(jnp.bfloat16)[None, :]
    return (weight_table, chosen, jnp.sum(weight).astype(jnp.float32))


def weigh_blocks(weight_table, chosen, deltas, changes):
    client_count = deltas.shape[0]
    local_rows = deltas.shape[1]
    columns = deltas.shape[2]
    moved_sum = jnp.dot(
        weight_table, deltas.reshape(client_count, -1), preferred_element_type=jnp.float32
    )
    varied = jnp.dot(chosen, changes.reshape(client_count, -1), preferred_element_type=jnp.float32)
    return ((moved_sum[0] + moved_sum[1]).reshape(local_rows, columns), varied)


def body(client_deltas, variate_deltas, params, variate, taking_part, counts):
    all_part, all_counts = (
        lax.all_gather(taking_part, ("clients", "shard"), axis=0, tiled=True),
        lax.all_gather(counts, ("clients", "shard"), axis=0, tiled=True),
    )
    weight_table, chosen, weight_total = weight_rows(all_part, all_counts)
    client_count = all_part.shape[0]
    summed, shifted = weigh_blocks(
        weight_table,
        chosen,
        lax.all_to_all(
            client_deltas, ("clients", "shard"), split_axis=1, concat_axis=0, tiled=True
        ),
        lax.all_to_all(
            variate_deltas, ("clients", "shard"), split_axis=1, concat_axis=0, tiled=True
        ),
    )
    new_params = params + summed / weight_total
    new_variate = variate + shifted / jnp.float32(client_count)
    client_params, client_variate = (
        lax.all_gather(new_params.astype(jnp.bfloat16), ("clients", "shard"), axis=0, tiled=True),
        lax.all_gather(new_variate.astype(jnp.bfloat16), ("clients", "shard"), axis=0, tiled=True),
    )
    return (new_params, new_variate, client_params, client_variate)


def solution(mesh):
    in_specs = (
        P(("clients", "shard"), None, None),
        P(("clients", "shard"), None, None),
        P(("clients", "shard"), None),
        P(("clients", "shard"), None),
        P(("clients", "shard")),
        P(("clients", "shard")),
    )
    out_specs = (P(("clients", "shard"), None), P(("clients", "shard"), None), P(), P())
    return jax.shard_map(body, mesh=mesh, in_specs=in_specs, out_specs=out_specs, check_vma=False)
```

profile of v0, /device:TPU:0, one launch (start us, length us, event | category | flops | bytes accessed | tf_op | source)
XLA Modules:
  0.0 211.8 jit_solution(14549116178163955121)
XLA Ops:
  0.6 2.3 %copy.14 = bf16[2,32,3584]{2,0,1:T(2,128)(2,1)} copy(bf16[2,32,3584]{2,1,0:T(8,128)(2,1)} %param.6) | data formatting | bytes 917504 | tf_op args[0]
  2.9 0.0 copy-start
  2.9 7.3 %all-to-all-start = ((bf16[2,32,3584]{2,0,1:T(2,128)(2,1)}), bf16[2,32,3584]{2,0,1:T(2,128)(2,1)S(1)}, u32[]{:S(2)}, u32[]{:S(2)}) async-start(bf16[2,32,3584]{2,0,1:T(2,128)(2,1)} %copy.14), calls=%async_computation | async-start | bytes 917504 | tf_op jit(solution)/shard_map/all_to_all | solution.py:37
  10.2 0.0 copy-done
  10.2 1.2 copy.15
  11.5 11.7 %all-to-all-done = bf16[2,32,3584]{2,0,1:T(2,128)(2,1)S(1)} async-done(((bf16[2,32,3584]{2,0,1:T(2,128)(2,1)}), bf16[2,32,3584]{2,0,1:T(2,128)(2,1)S(1)}, u32[]{:S(2)}, u32[]{:S(2)}) %all-to-all-start) | async-done | bytes 458784 | tf_op jit(solution)/shard_map/all_to_all | solution.py:37
  23.2 4.1 %all-to-all-start.1 = ((bf16[2,32,3584]{2,0,1:T(2,128)(2,1)}), bf16[2,32,3584]{2,0,1:T(2,128)(2,1)S(1)}, u32[]{:S(2)}, u32[]{:S(2)}) async-start(bf16[2,32,3584]{2,0,1:T(2,128)(2,1)} %copy.15), calls=%async_computation.1 | async-start | bytes 917504 | tf_op jit(solution)/shard_map/all_to_all | solution.py:40
  27.3 0.0 copy-start.3
  27.3 0.6 copy-done.3
  27.9 0.2 dynamic-update-slice
  28.1 0.0 copy-start.4
  28.1 0.7 copy-done.4
  28.8 0.2 dynamic-update-slice.1
  28.9 40.4 %all-reduce.2 = (s32[64]{0:T(128)S(1)}, s32[64]{0:T(128)S(1)}) all-reduce(s32[64]{0:T(128)S(1)} %dynamic-update-slice, s32[64]{0:T(128)S(1)} %dynamic-update-slice.1), channel_id=1, replica_groups=mesh['clients'=8,'shard'=4] {'clients','shard'}, use_global_device_ids=true, to_apply=%add | all-reduce | flops 128 | bytes 1024
  69.4 0.6 convert_bitcast_fusion.2
  70.7 0.2 reshape.22
  70.9 0.0 all-to-all-done.1
  70.9 0.2 reshape.23
  71.1 0.2 convolution_reduce_fusion
  71.3 0.0 copy-start.1
  71.3 0.2 fusion
  71.4 0.5 copy-done.1
  72.0 0.6 convert_bitcast_fusion.1
  72.6 70.0 %all-gather = bf16[32,1,3584]{2,1,0:T(2,128)(2,1)S(1)} all-gather(bf16[1,1,3584]{2,1,0:T(2,128)(2,1)S(1)} %get-tuple-element.8), channel_id=1, replica_groups=mesh['clients'=8,'shard'=4] {'clients','shard'}, dimensions={0}, use_global_device_ids=true | all-gather | bytes 236544 | tf_op jit(solution)/shard_map/all_gather | solution.py:47
  142.6 0.0 copy-start.2
  142.6 0.7 copy.21
  143.3 0.0 copy-done.2
  143.3 0.6 convert_bitcast_fusion
  143.9 67.2 %all-gather.1 = bf16[32,1,3584]{2,1,0:T(2,128)(2,1)S(1)} all-gather(bf16[1,1,3584]{2,1,0:T(2,128)(2,1)S(1)} %get-tuple-element.6), channel_id=1, replica_groups=mesh['clients'=8,'shard'=4] {'clients','shard'}, dimensions={0}, use_global_device_ids=true | all-gather | bytes 236544 | tf_op jit(solution)/shard_map/all_gather | solution.py:48
  211.1 0.7 copy.20
  (4 shorter events, 0.0 us)
Async XLA Ops:
  2.9 7.3 %copy-start = (bf16[2,32,3584]{2,1,0:T(8,128)(2,1)S(1)}, bf16[2,32,3584]{2,1,0:T(8,128)(2,1)}, u32[]{:S(2)}) copy-start(bf16[2,32,3584]{2,1,0:T(8,128)(2,1)} %param.7) | copy-start | bytes 1376260
  2.9 20.3 %all-to-all-start = ((bf16[2,32,3584]{2,0,1:T(2,128)(2,1)}), bf16[2,32,3584]{2,0,1:T(2,128)(2,1)S(1)}, u32[]{:S(2)}, u32[]{:S(2)}) async-start(bf16[2,32,3584]{2,0,1:T(2,128)(2,1)} %copy.14), calls=%async_computation | async-start | bytes 917504 | tf_op jit(solution)/shard_map/all_to_all | solution.py:37
  23.2 47.7 %all-to-all-start.1 = ((bf16[2,32,3584]{2,0,1:T(2,128)(2,1)}), bf16[2,32,3584]{2,0,1:T(2,128)(2,1)S(1)}, u32[]{:S(2)}, u32[]{:S(2)}) async-start(bf16[2,32,3584]{2,0,1:T(2,128)(2,1)} %copy.15), calls=%async_computation.1 | async-start | bytes 917504 | tf_op jit(solution)/shard_map/all_to_all | solution.py:40
  27.3 0.7 copy-start.3
  28.1 0.7 copy-start.4
  71.3 0.7 copy-start.1
  142.6 0.7 copy-start.2
where the time goes:
time: 213 us; the launch traced here: 212 us
  blocking collectives  178 us (84%)
  waiting for transfers between devices  11.7 us (5%)
  starting transfers between devices  11.4 us (5%)
  local copies, waits for them, and re-layouts  7.49 us (4%)
    all_gather x1, blocking collectives, body(): lax.all_gather(new_params.astype(jnp.bfloat16), ('clients', 'shard'), axi...  70 us
    all_gather x1, blocking collectives, body(): lax.all_gather(new_variate.astype(jnp.bfloat16), ('clients', 'shard'), ax...  67.2 us
    unnamed x1, blocking collectives  40.4 us
    all_to_all x1, waiting for transfers between devices, body(): lax.all_to_all(client_deltas, ('clients', 'shard'), split_axis=1, concat_...  11.7 us
    all_to_all x1, starting transfers between devices, body(): lax.all_to_all(client_deltas, ('clients', 'shard'), split_axis=1, concat_...  7.33 us
    unnamed x18, local copies, waits for them, and re-layouts  7.14 us
  transfers between devices with their start and end apart: 2, of which 1 were waited for; matrix products, arithmetic and copies ran while one was open for 1% of the time, Pallas kernels for 0%

commit v1 on v0

--- a/solution.py
+++ b/solution.py
@@ -2,6 +2,13 @@
 import jax.numpy as jnp
 from jax import lax
 from jax.sharding import PartitionSpec as P
+
+
+def swap_blocks(block, axis, split, join):
+    size = lax.axis_size(axis)
+    blocks = jnp.stack(jnp.split(block, size, axis=split), axis=0)
+    blocks = lax.all_to_all(blocks, axis, split_axis=0, concat_axis=0)
+    return jnp.concatenate(blocks, axis=join)
 
 
 def weight_rows(taking_part, counts):
@@ -34,9 +41,7 @@
     summed, shifted = weigh_blocks(
         weight_table,
         chosen,
-        lax.all_to_all(
-            client_deltas, ("clients", "shard"), split_axis=1, concat_axis=0, tiled=True
-        ),
+        swap_blocks(client_deltas, ("clients", "shard"), 1, 0),
         lax.all_to_all(
             variate_deltas, ("clients", "shard"), split_axis=1, concat_axis=0, tiled=True
         ),

time: 213 us -> 227 us (1.066)
  local copies, waits for them, and re-layouts: 7.49 us -> 28 us
  waiting for transfers between devices: 11.7 us -> 0.01 us
  blocking collectives: 178 us -> 182 us
    unnamed x18 -> x50, local copies, waits for them, and re-layouts: 7.14 us -> 24.6 us
    all_to_all x1, waiting for transfers between devices: 11.7 us -> 0.01 us  [swap_blocks(): blocks = lax.all_to_all(blocks, axis, split_axis=0, concat_axis=0)]
    all_gather x1, blocking collectives: 70 us -> 73.4 us  [body(): lax.all_gather(new_params.astype(jnp.bfloat16), ('clients', 'shard'), axi...]
    split x0 -> x2, local copies, waits for them, and re-layouts: none -> 2.5 us  [swap_blocks(): blocks = jnp.stack(jnp.split(block, size, axis=split), axis=0)]
  transfers between devices with their start and end apart: 2 -> 2, of which waited for: 1 -> 0; matrix products, arithmetic and copies ran while one was open for 1% -> 2% of each run, Pallas kernels for 0% -> 0%
where the time goes in v1:
time: 227 us; the launch traced here: 226 us
  blocking collectives  182 us (80%)
  local copies, waits for them, and re-layouts  28 us (12%)
  starting transfers between devices  12 us (5%)
    all_gather x1, blocking collectives, body(): lax.all_gather(new_params.astype(jnp.bfloat16), ('clients', 'shard'), axi...  73.4 us
    all_gather x1, blocking collectives, body(): lax.all_gather(new_variate.astype(jnp.bfloat16), ('clients', 'shard'), ax...  68.5 us
    unnamed x1, blocking collectives  40.4 us
    unnamed x50, local copies, waits for them, and re-layouts  24.6 us
    all_to_all x1, starting transfers between devices, swap_blocks(): blocks = lax.all_to_all(blocks, axis, split_axis=0, concat_axis=0)  7.33 us
    all_to_all x1, starting transfers between devices, body(): lax.all_to_all(variate_deltas, ('clients', 'shard'), split_axis=1, concat...  4.65 us
  transfers between devices with their start and end apart: 2, of which 0 were waited for; matrix products, arithmetic and copies ran while one was open for 2% of the time, Pallas kernels for 0%

profile of v1, /device:TPU:0, one launch (start us, length us, event | category | flops | bytes accessed | tf_op | source)
XLA Modules:
  0.0 226.0 jit_solution(6104810912641985082)
XLA Ops:
  0.6 0.0 copy-start
  0.6 2.1 fusion.10
  2.7 0.0 copy-done
  2.7 0.4 fusion.9
  3.2 0.6 constant_dynamic-update-slice_fusion.31
  3.8 0.6 constant_dynamic-update-slice_fusion.30
  4.4 0.6 constant_dynamic-update-slice_fusion.29
  5.0 0.6 constant_dynamic-update-slice_fusion.28
  5.6 0.6 constant_dynamic-update-slice_fusion.27
  6.2 0.6 constant_dynamic-update-slice_fusion.26
  6.8 0.6 constant_dynamic-update-slice_fusion.25
  7.4 0.6 constant_dynamic-update-slice_fusion.24
  8.1 0.6 constant_dynamic-update-slice_fusion.23
  8.7 0.6 constant_dynamic-update-slice_fusion.22
  9.3 0.6 constant_dynamic-update-slice_fusion.21
  9.9 0.6 constant_dynamic-update-slice_fusion.20
  10.5 0.6 constant_dynamic-update-slice_fusion.19
  11.1 0.6 constant_dynamic-update-slice_fusion.18
  11.7 0.6 constant_dynamic-update-slice_fusion.17
  12.3 0.6 constant_dynamic-update-slice_fusion.16
  13.0 0.6 constant_dynamic-update-slice_fusion.15
  13.6 0.6 constant_dynamic-update-slice_fusion.14
  14.2 0.6 constant_dynamic-update-slice_fusion.13
  14.8 0.6 constant_dynamic-update-slice_fusion.12
  15.4 0.6 constant_dynamic-update-slice_fusion.11
  16.0 0.6 constant_dynamic-update-slice_fusion.10
  16.6 0.6 constant_dynamic-update-slice_fusion.9
  17.3 0.6 constant_dynamic-update-slice_fusion.8
  17.9 0.6 constant_dynamic-update-slice_fusion.7
  18.5 0.6 constant_dynamic-update-slice_fusion.6
  19.1 0.6 constant_dynamic-update-slice_fusion.5
  19.7 0.6 constant_dynamic-update-slice_fusion.4
  20.3 0.6 constant_dynamic-update-slice_fusion.3
  20.9 0.6 constant_dynamic-update-slice_fusion.2
  21.6 0.6 constant_dynamic-update-slice_fusion.1
  22.2 0.6 constant_dynamic-update-slice_fusion
  22.8 0.0 copy-start.1
  22.8 7.3 %all-to-all-start = ((bf16[32,2,1,3584]{3,1,2,0:T(2,128)(2,1)}), bf16[32,2,1,3584]{3,1,2,0:T(2,128)(2,1)S(1)}, u32[]{:S(2)}, u32[]{:S(2)}) async-start(bf16[32,2,1,3584]{3,1,2,0:T(2,128)(2,1)} %constant_dynamic-update-slice_fusion), calls=%async_computation | async-start | bytes 917504 | tf_op jit(solution)/shard_map/all_to_all | solution.py:10
  30.1 0.0 copy-start.4
  30.2 0.6 copy-done.4
  30.8 0.2 dynamic-update-slice
  31.0 0.7 copy-done.5
  31.6 0.2 dynamic-update-slice.1
  31.8 40.4 %all-reduce.2 = (s32[64]{0:T(128)S(1)}, s32[64]{0:T(128)S(1)}) all-reduce(s32[64]{0:T(128)S(1)} %dynamic-update-slice, s32[64]{0:T(128)S(1)} %dynamic-update-slice.1), channel_id=1, replica_groups=mesh['clients'=8,'shard'=4] {'clients','shard'}, use_global_device_ids=true, to_apply=%add | all-reduce | flops 128 | bytes 1024
  72.3 0.6 convert_bitcast_fusion.2
  73.6 0.0 copy-done.1
  73.6 1.2 copy.136
  74.8 0.0 all-to-all-done
  74.8 4.7 %all-to-all-start.1 = ((bf16[2,32,3584]{2,0,1:T(2,128)(2,1)}), bf16[2,32,3584]{2,0,1:T(2,128)(2,1)S(1)}, u32[]{:S(2)}, u32[]{:S(2)}) async-start(bf16[2,32,3584]{2,0,1:T(2,128)(2,1)} %copy.136), calls=%async_computation.1 | async-start | bytes 917504 | tf_op jit(solution)/shard_map/all_to_all | solution.py:45
  79.5 0.2 reshape_reshape.3
  79.7 0.0 copy-start.2
  79.7 0.2 fusion
  79.8 0.5 copy-done.2
  80.4 0.6 convert_bitcast_fusion.1
  81.0 73.4 %all-gather = bf16[32,1,3584]{2,1,0:T(2,128)(2,1)S(1)} all-gather(bf16[1,1,3584]{2,1,0:T(2,128)(2,1)S(1)} %get-tuple-element.8), channel_id=1, replica_groups=mesh['clients'=8,'shard'=4] {'clients','shard'}, dimensions={0}, use_global_device_ids=true | all-gather | bytes 236544 | tf_op jit(solution)/shard_map/all_gather | solution.py:52
  154.4 0.7 copy.268
  155.1 0.0 all-to-all-done.1
  155.1 0.2 reshape.18
  155.3 0.2 convolution_reduce_fusion
  155.4 0.0 copy-start.3
  155.5 0.7 copy-done.3
  156.2 0.6 convert_bitcast_fusion
  156.8 68.5 %all-gather.1 = bf16[32,1,3584]{2,1,0:T(2,128)(2,1)S(1)} all-gather(bf16[1,1,3584]{2,1,0:T(2,128)(2,1)S(1)} %get-tuple-element.6), channel_id=1, replica_groups=mesh['clients'=8,'shard'=4] {'clients','shard'}, dimensions={0}, use_global_device_ids=true | all-gather | bytes 236544 | tf_op jit(solution)/shard_map/all_gather | solution.py:53
  225.3 0.7 copy.267
  (5 shorter events, 0.0 us)
Async XLA Ops:
  0.6 2.1 copy-start
  22.8 50.8 %copy-start.1 = (bf16[2,32,3584]{2,1,0:T(8,128)(2,1)S(1)}, bf16[2,32,3584]{2,1,0:T(8,128)(2,1)}, u32[]{:S(2)}) copy-start(bf16[2,32,3584]{2,1,0:T(8,128)(2,1)} %param.7) | copy-start | bytes 1376260
  22.8 52.0 %all-to-all-start = ((bf16[32,2,1,3584]{3,1,2,0:T(2,128)(2,1)}), bf16[32,2,1,3584]{3,1,2,0:T(2,128)(2,1)S(1)}, u32[]{:S(2)}, u32[]{:S(2)}) async-start(bf16[32,2,1,3584]{3,1,2,0:T(2,128)(2,1)} %constant_dynamic-update-slice_fusion), calls=%async_computation | async-start | bytes 917504 | tf_op jit(solution)/shard_map/all_to_all | solution.py:10
  30.1 0.7 copy-start.4
  31.0 0.7 copy-start.5
  74.8 80.3 %all-to-all-start.1 = ((bf16[2,32,3584]{2,0,1:T(2,128)(2,1)}), bf16[2,32,3584]{2,0,1:T(2,128)(2,1)S(1)}, u32[]{:S(2)}, u32[]{:S(2)}) async-start(bf16[2,32,3584]{2,0,1:T(2,128)(2,1)} %copy.136), calls=%async_computation.1 | async-start | bytes 917504 | tf_op jit(solution)/shard_map/all_to_all | solution.py:45
  79.7 0.7 copy-start.2
  155.4 0.7 copy-start.3
